TPU v7x, 32 devices: a whole 2x2x4 slice. The times are simulated.
32 devices in a mesh: ga: 2 (over x), ta: 4 (over y, core), gy: 4 (over z).
Axes of the slice: x: 2, y: 2, z: 4, core: 2. Of those that a mesh axis runs over, the one named last changes fastest.
Arguments:
- clip: bfloat16 [32, 16, 64, 512], P(('ga', 'ta'), 'gy'), parts along dimension 0, may hold values from -6 to 6
- w_space: bfloat16 [3, 3, 512, 512], replicated, may hold values from -0.09375 to 0.09375
- w_time: bfloat16 [3, 512, 512], replicated, may hold values from -0.15625 to 0.15625
- w_qkv: bfloat16 [512, 1536], replicated, may hold values from -0.61871843 to 0.61871843
- w_out: bfloat16 [512, 512], replicated, may hold values from -0.25 to 0.25
- norm_gain: float32 [512], replicated, may hold values from 0.1 to 1.9
Outputs:
- block_out: bfloat16 [32, 16, 64, 512], P(('ga', 'ta'), 'gy'), parts along dimension 0
There are 2 independent parts, one for each index of `ga`. A program takes and returns all parts, laid end to end along the dimension named above; an argument that names none is the same for every part. Nothing has to cross between parts.
All inputs are finite; a program needn't handle non-finite values.
Results may differ from a plain program's by a relative error of at most 0.0085.
Values may be sent and summed in bfloat16 or wider, within the bound.
No kernel may reach another device: no remote copies, remote signals or barrier semaphores. Data moves between devices by JAX's collectives and lax.ppermute only.
A program may use at most 64 MiB of HBM per device.

v0:
```python
import jax
import jax.numpy as jnp
from jax import lax
from jax.sharding import PartitionSpec as P

HEADS = 8


def padded_2(block, sides, width):
    for axis, dim in sides:
        count = lax.axis_size(axis)
        forward = [(i, i + 1) for i in range(count - 1)]
        backward = [(target, source) for source, target in forward]
        low = lax.ppermute(
            lax.slice_in_dim(block, block.shape[dim] - width, None, axis=dim), axis, forward
        )
        high = lax.ppermute(lax.slice_in_dim(block, 0, width, axis=dim), axis, backward)
        block = jnp.concatenate([low, block, high], axis=dim)
    return block


def from_behind(array, axis, by):
    devices = lax.axis_size(axis)
    pairs = [(i, i + by) for i in range(devices) if 0 <= i + by < devices]
    return lax.ppermute(array, axis, pairs)


def conv_space(padded, w_space, height, width):
    channels = padded.shape[-1]
    total = jnp.zeros(padded.shape[:1] + (height, width, channels), jnp.float32)
    for row_off in range(3):
        for col_off in range(3):
            window = padded[:, row_off : row_off + height, col_off : col_off + width, :]
            product = jnp.dot(
                window.reshape(-1, channels),
                w_space[row_off, col_off],
                preferred_element_type=jnp.float32,
            )
            total = total + product.reshape(total.shape)
    return total


def temporal_mix(clip, hidden, earlier, w_time, norm_gain):
    channels = clip.shape[-1]
    frames = hidden.shape[0]
    joined = jnp.concatenate([earlier, hidden], axis=0)
    total = jnp.zeros(hidden.shape, jnp.float32)
    for tap_index in range(3):
        window = joined[2 - tap_index : 2 - tap_index + frames]
        product = jnp.dot(
            window.reshape(-1, channels), w_time[tap_index], preferred_element_type=jnp.float32
        )
        total = total + product.reshape(hidden.shape)
    mixed = (clip.astype(jnp.float32) + total).astype(jnp.bfloat16)
    wide = mixed.astype(jnp.float32)
    scale = lax.rsqrt(jnp.mean(wide * wide, axis=-1, keepdims=True) + 1e-06)
    normed = (wide * scale * norm_gain).astype(jnp.bfloat16)
    return (mixed, normed)


def project(normed, w_qkv):
    channels = normed.shape[-1]
    flattened = jnp.dot(
        normed.reshape(-1, channels), w_qkv, preferred_element_type=jnp.float32
    ).astype(jnp.bfloat16)
    joined = flattened.reshape(normed.shape[:-1] + (3 * channels,))
    return (
        joined[..., :channels],
        joined[..., channels : 2 * channels],
        joined[..., 2 * channels :],
    )


def attend(queries, keyset, valueset, heads):
    frames, rows, cols, channels = queries.shape
    head_dim = channels // heads
    shape = (frames, rows, cols, heads, head_dim)
    scores = jnp.einsum(
        "frwhd,grwhd->rwhfg",
        queries.reshape(shape),
        keyset.reshape(shape),
        preferred_element_type=jnp.float32,
    )
    scores = scores * (1.0 / head_dim**0.5)
    peak = jnp.max(scores, axis=-1, keepdims=True)
    expo = jnp.exp(scores - peak)
    probs = (expo / jnp.sum(expo, axis=-1, keepdims=True)).astype(jnp.bfloat16)
    output = jnp.einsum(
        "rwhfg,grwhd->frwhd", probs, valueset.reshape(shape), preferred_element_type=jnp.float32
    )
    return output.reshape(queries.shape).astype(jnp.bfloat16)


def attend_back(queries, keyset, valueset):
    output = attend(queries, keyset, valueset, HEADS)
    return lax.all_to_all(output, "ta", split_axis=0, concat_axis=2, tiled=True)


def per_device(clip, w_space, w_time, w_qkv, w_out, norm_gain):
    frames, height, width, channels = clip.shape
    rimmed = padded_2(clip, (("gy", 1),), 1)
    padded = jnp.pad(rimmed, ((0, 0), (0, 0), (1, 1), (0, 0)))
    hidden = jax.nn.silu(conv_space(padded, w_space, height, width)).astype(jnp.bfloat16)
    earlier = from_behind(hidden[-2:], "ta", 1)
    mixed, normed = temporal_mix(clip, hidden, earlier, w_time, norm_gain)
    queries, keyset, valueset = project(
        lax.all_to_all(normed, "ta", split_axis=2, concat_axis=0, tiled=True), w_qkv
    )
    attended = attend_back(queries, keyset, valueset)
    projected = jnp.dot(
        attended.reshape(-1, channels), w_out, preferred_element_type=jnp.float32
    ).reshape(clip.shape)
    return (mixed.astype(jnp.float32) + projected).astype(jnp.bfloat16)


def solution(mesh):
    in_specs = (P(("ga", "ta"), "gy", None, None), P(), P(), P(), P(), P())
    out_specs = P(("ga", "ta"), "gy", None, None)
    return jax.shard_map(
        per_device, mesh=mesh, in_specs=in_specs, out_specs=out_specs, check_vma=False
    )
```

profile of v0, /device:TPU:0, one launch (start us, length us, event | category | flops | bytes accessed | tf_op | source)
XLA Modules:
  0.0 112.8 jit_solution(17687621035857392692)
XLA Ops:
  0.0 0.0 copy-start
  0.0 1.2 %fusion.79 = (bf16[4,1,64,512]{3,2,1,0:T(8,128)(2,1)S(1)}, bf16[4,1,64,512]{3,2,1,0:T(8,128)(2,1)S(1)}) fusion(bf16[4,4,64,512]{3,2,1,0:T(8,128)(2,1)} %param.6), kind=kLoop, calls=%fused_computation.87 | loop fusion | bytes 1048576 | tf_op jit(solution)/shard_map/slice | solution.py:15
  1.2 5.0 %collective-permute-start = (bf16[4,1,64,512]{3,2,1,0:T(8,128)(2,1)S(1)}, bf16[4,1,64,512]{3,2,1,0:T(8,128)(2,1)S(1)}, u32[]{:S(2)}, u32[]{:S(2)}) collective-permute-start(bf16[4,1,64,512]{3,2,1,0:T(8,128)(2,1)S(1)} %get-tuple-element.8), channel_id=1, source_target_pairs={{0,1},{1,2},{2,3},{4,5},{5,6},{6,7},{8,9},{9,10},{10,11},{12,13},{... | collective-permute-start | bytes 786440 | tf_op jit(solution)/shard_map/ppermute | solution.py:14
  6.2 0.0 copy-start.2
  6.2 1.4 %collective-permute-start.1 = (bf16[4,1,64,512]{3,2,1,0:T(8,128)(2,1)S(1)}, bf16[4,1,64,512]{3,2,1,0:T(8,128)(2,1)S(1)}, u32[]{:S(2)}, u32[]{:S(2)}) collective-permute-start(bf16[4,1,64,512]{3,2,1,0:T(8,128)(2,1)S(1)} %get-tuple-element.9), channel_id=1, source_target_pairs={{1,0},{2,1},{3,2},{5,4},{6,5},{7,6},{9,8},{10,9},{11,10},{13,12},{... | collective-permute-start | bytes 786440 | tf_op jit(solution)/shard_map/ppermute | solution.py:17
  7.6 0.0 copy-start.4
  7.6 2.2 %fusion.55 = f32[4,4,64,512]{3,2,1,0:T(8,128)S(1)} fusion(bf16[4,4,64,512]{3,2,1,0:T(8,128)(2,1)} %param.6, bf16[3,3,512,512]{3,2,1,0:T(8,128)(2,1)} %param.7), kind=kOutput, calls=%fused_computation.62 | convolution fusion | flops 536870912 | bytes 3670016 | tf_op jit(solution)/shard_map/dot_general | solution.py:34
  9.8 1.9 %collective-permute-done = bf16[4,1,64,512]{3,2,1,0:T(8,128)(2,1)S(1)} collective-permute-done((bf16[4,1,64,512]{3,2,1,0:T(8,128)(2,1)S(1)}, bf16[4,1,64,512]{3,2,1,0:T(8,128)(2,1)S(1)}, u32[]{:S(2)}, u32[]{:S(2)}) %collective-permute-start) | collective-permute-done | bytes 262176 | tf_op jit(solution)/shard_map/ppermute | solution.py:14
  11.7 4.3 %collective-permute-done.1 = bf16[4,1,64,512]{3,2,1,0:T(8,128)(2,1)S(1)} collective-permute-done((bf16[4,1,64,512]{3,2,1,0:T(8,128)(2,1)S(1)}, bf16[4,1,64,512]{3,2,1,0:T(8,128)(2,1)S(1)}, u32[]{:S(2)}, u32[]{:S(2)}) %collective-permute-start.1) | collective-permute-done | bytes 262176 | tf_op jit(solution)/shard_map/ppermute | solution.py:17
  16.0 0.0 copy-done.2
  16.0 0.9 fusion.22
  16.9 0.0 copy-done.4
  16.9 0.7 fusion.35
  17.6 0.7 fusion.37
  18.3 0.7 fusion.39
  19.0 0.7 fusion.41
  19.8 0.7 fusion.43
  20.5 0.7 fusion.23
  21.2 0.7 fusion.27
  21.9 0.0 copy-start.5
  21.9 1.4 %multiply_convert_fusion = bf16[4,4,64,512]{3,2,1,0:T(8,128)(2,1)S(1)} fusion(f32[4,4,64,512]{3,2,1,0:T(8,128)S(1)} %fusion.27, f32[4,4,64,512]{3,2,1,0:T(8,128)S(1)} %fusion.35, f32[4,4,64,512]{3,2,1,0:T(8,128)S(1)} %fusion.37, f32[4,4,64,512]{3,2,1,0:T(8,128)S(1)} %fusion.55, f32[4,4,64,512]{3,2,1,0:T(8,128)S(1)} %fusion.39, ...), kind=kOutput, calls=%fused_computation.25 | convolution fusion | flops 543686656 | bytes 19398656 | tf_op jit(solution)/shard_map/dot_general | solution.py:34
  23.4 1.3 %collective-permute-start.2 = (bf16[2,4,64,512]{3,2,1,0:T(8,128)(2,1)S(1)}, bf16[2,4,64,512]{3,2,1,0:T(8,128)(2,1)S(1)}, u32[]{:S(2)}, u32[]{:S(2)}) collective-permute-start(bf16[2,4,64,512]{3,2,1,0:T(8,128)(2,1)S(1)} %slice.124), channel_id=1, source_target_pairs={{0,4},{4,8},{8,12},{1,5},{5,9},{9,13},{2,6},{6,10},{10,14},{3,7},{... | collective-permute-start | bytes 1572872 | tf_op jit(solution)/shard_map/ppermute | solution.py:25
  24.7 0.0 copy-done.5
  24.7 0.7 fusion.49
  25.4 0.8 collective-permute-done.2
  26.2 0.7 fusion.45
  26.9 0.0 copy-start.6
  26.9 1.0 fusion.5
  27.9 0.0 copy-done.6
  28.0 0.3 fusion.7
  28.3 0.8 copy.22
  29.1 24.7 %all_to_all.30 = bf16[4,4,64,512]{3,1,0,2:T(4,128)(2,1)S(1)} all-to-all(bf16[4,4,64,512]{3,1,0,2:T(4,128)(2,1)S(1)} %copy.22), channel_id=1, replica_groups=mesh['ga'=2,'ta'=4,'gy'=4] {'ta'}, dimensions={2} | all-to-all | bytes 2097152 | tf_op jit(solution)/shard_map/all_to_all | solution.py:107
  53.8 0.6 copy.23
  54.4 0.1 copy.24
  54.4 0.0 copy-done
  54.5 1.8 %convolution_convert_fusion = bf16[1024,1536]{1,0:T(8,128)(2,1)S(1)} fusion(bf16[1024,512]{1,0:T(8,128)(2,1)S(1)} %bitcast.119, bf16[512,1536]{1,0:T(8,128)(2,1)S(1)} %copy-done), kind=kOutput, calls=%fused_computation.5 | convolution fusion | flops 1612185600 | bytes 5767168 | tf_op jit(solution)/shard_map/dot_general | solution.py:63
  56.3 1.7 %fusion.78 = (bf16[16,4,16,512]{3,2,1,0:T(8,128)(2,1)S(1)}, bf16[16,4,16,512]{3,2,1,0:T(8,128)(2,1)}, bf16[16,4,16,512]{3,2,1,0:T(8,128)(2,1)}) fusion(bf16[16,4,16,1536]{3,2,1,0:T(8,128)(2,1)S(1)} %bitcast.117), kind=kLoop, calls=%fused_computation.86 | loop fusion | bytes 6291456 | tf_op jit(solution)/shard_map/slice | solution.py:70
  57.9 2.1 %reshape.84 = bf16[16,4,16,8,64]{4,3,2,1,0:T(8,128)(2,1)} reshape(bf16[16,4,16,512]{3,2,1,0:T(8,128)(2,1)S(1)} %get-tuple-element.5) | data formatting | bytes 2097152 | tf_op jit(solution)/shard_map/reshape | solution.py:89
  60.0 2.8 %reshape.86 = bf16[16,4,16,8,64]{4,3,2,1,0:T(8,128)(2,1)S(1)} reshape(bf16[16,4,16,512]{3,2,1,0:T(8,128)(2,1)} %get-tuple-element.6) | data formatting | bytes 2097152 | tf_op jit(solution)/shard_map/reshape | solution.py:81
  62.8 3.9 %reshape.85 = bf16[16,4,16,8,64]{4,3,2,1,0:T(8,128)(2,1)} reshape(bf16[16,4,16,512]{3,2,1,0:T(8,128)(2,1)} %get-tuple-element.7) | data formatting | bytes 2097152 | tf_op jit(solution)/shard_map/reshape | solution.py:80
  66.7 4.1 %fusion.11 = f32[4,16,8,16,16]{3,4,2,1,0:T(8,128)S(1)} fusion(bf16[16,4,16,8,64]{4,3,2,1,0:T(8,128)(2,1)S(1)} %reshape.86, bf16[16,4,16,8,64]{4,3,2,1,0:T(8,128)(2,1)} %reshape.85), kind=kOutput, calls=%fused_computation.18 | convolution fusion | flops 16777216 | bytes 2621440 | tf_op jit(solution)/shard_map/frwhd,grwhd->rwhfg/dot_general | solution.py:78
  70.8 0.0 copy-start.3
  70.8 17.7 %fusion.80 = (f32[4,16,8,16]{3,2,1,0:T(8,128)S(1)}, f32[4,16,8,16,16]{3,4,2,1,0:T(8,128)S(1)}) fusion(f32[4,16,8,16,16]{3,4,2,1,0:T(8,128)S(1)} %fusion.11), kind=kOutput, calls=%fused_computation.88 | output fusion | flops 524303 | bytes 1081344 | tf_op jit(solution)/shard_map/sub | solution.py:86
  88.6 0.0 copy-done.3
  88.6 1.7 %convert_bitcast_fusion = bf16[16,4,16,8,64]{4,0,3,2,1:T(8,128)(2,1)S(1)} fusion(f32[4,16,8,16,16]{3,4,2,1,0:T(8,128)S(1)} %get-tuple-element.13, f32[4,16,8,16]{3,2,1,0:T(8,128)S(1)} %get-tuple-element.12, bf16[16,4,16,8,64]{4,3,2,1,0:T(8,128)(2,1)S(1)} %copy-done.3), kind=kOutput, calls=%fused_computation.21 | convolution fusion | flops 17563648 | bytes 2654208 | tf_op jit(solution)/shard_map/rwhfg,grwhd->frwhd/dot_general | solution.py:88
  90.3 0.5 copy.29
  90.9 2.0 %convert_element_type.45 = bf16[16,4,16,512]{3,2,1,0:T(8,128)(2,1)} reshape(bf16[16,4,16,8,64]{4,3,2,1,0:T(8,128)(2,1)S(1)} %copy.29) | data formatting | bytes 2097152 | tf_op jit(solution)/shard_map/convert_element_type | solution.py:91
  92.9 0.0 copy-start.7
  92.9 18.0 %all_to_all.31 = bf16[16,4,16,512]{3,2,1,0:T(8,128)(2,1)S(1)} all-to-all(bf16[16,4,16,512]{3,2,1,0:T(8,128)(2,1)} %convert_element_type.45), channel_id=1, replica_groups=mesh['ga'=2,'ta'=4,'gy'=4] {'ta'}, dimensions={0} | all-to-all | bytes 2097152 | tf_op jit(solution)/shard_map/all_to_all | solution.py:96
  111.0 0.1 copy.30
  111.1 0.0 copy-start.1
  111.1 0.0 copy-done.7
  111.1 1.7 %fusion.8 = bf16[4,4,64,512]{3,2,1,0:T(8,128)(2,1)} fusion(bf16[4,4,64,512]{3,2,1,0:T(8,128)(2,1)S(1)} %get-tuple-element.11, bf16[4,4,64,512]{3,2,1,0:T(8,128)(2,1)S(1)} %bitcast.118, bf16[512,512]{1,0:T(8,128)(2,1)S(1)} %copy-done.7), kind=kOutput, calls=%fused_computation.15 | convolution fusion | flops 538443776 | bytes 3670016 | tf_op jit(solution)/shard_map/dot_general | solution.py:110
  112.7 0.0 copy-done.1
  (2 shorter events, 0.0 us)
Async XLA Ops:
  0.0 54.4 %copy-start = (bf16[512,1536]{1,0:T(8,128)(2,1)S(1)}, bf16[512,1536]{1,0:T(8,128)(2,1)}, u32[]{:S(2)}) copy-start(bf16[512,1536]{1,0:T(8,128)(2,1)} %param.9) | copy-start | bytes 4718596
  1.2 10.5 %collective-permute-start = (bf16[4,1,64,512]{3,2,1,0:T(8,128)(2,1)S(1)}, bf16[4,1,64,512]{3,2,1,0:T(8,128)(2,1)S(1)}, u32[]{:S(2)}, u32[]{:S(2)}) collective-permute-start(bf16[4,1,64,512]{3,2,1,0:T(8,128)(2,1)S(1)} %get-tuple-element.8), channel_id=1, source_target_pairs={{0,1},{1,2},{2,3},{4,5},{5,6},{6,7},{8,9},{9,10},{10,11},{12,13},{... | collective-permute-start | bytes 786440 | tf_op jit(solution)/shard_map/ppermute | solution.py:14
  6.2 9.8 %copy-start.2 = (bf16[4,4,64,512]{3,2,1,0:T(8,128)(2,1)S(1)}, bf16[4,4,64,512]{3,2,1,0:T(8,128)(2,1)}, u32[]{:S(2)}) copy-start(bf16[4,4,64,512]{3,2,1,0:T(8,128)(2,1)} %param.6) | copy-start | bytes 3145732
  6.2 9.8 %collective-permute-start.1 = (bf16[4,1,64,512]{3,2,1,0:T(8,128)(2,1)S(1)}, bf16[4,1,64,512]{3,2,1,0:T(8,128)(2,1)S(1)}, u32[]{:S(2)}, u32[]{:S(2)}) collective-permute-start(bf16[4,1,64,512]{3,2,1,0:T(8,128)(2,1)S(1)} %get-tuple-element.9), channel_id=1, source_target_pairs={{1,0},{2,1},{3,2},{5,4},{6,5},{7,6},{9,8},{10,9},{11,10},{13,12},{... | collective-permute-start | bytes 786440 | tf_op jit(solution)/shard_map/ppermute | solution.py:17
  7.6 9.3 %copy-start.4 = (bf16[3,3,512,512]{3,2,1,0:T(8,128)(2,1)S(1)}, bf16[3,3,512,512]{3,2,1,0:T(8,128)(2,1)}, u32[]{:S(2)}) copy-start(bf16[3,3,512,512]{3,2,1,0:T(8,128)(2,1)} %param.7) | copy-start | bytes 14155780
  21.9 2.8 %copy-start.5 = (bf16[3,512,512]{2,1,0:T(8,128)(2,1)S(1)}, bf16[3,512,512]{2,1,0:T(8,128)(2,1)}, u32[]{:S(2)}) copy-start(bf16[3,512,512]{2,1,0:T(8,128)(2,1)} %param.8) | copy-start | bytes 4718596
  23.4 2.8 %collective-permute-start.2 = (bf16[2,4,64,512]{3,2,1,0:T(8,128)(2,1)S(1)}, bf16[2,4,64,512]{3,2,1,0:T(8,128)(2,1)S(1)}, u32[]{:S(2)}, u32[]{:S(2)}) collective-permute-start(bf16[2,4,64,512]{3,2,1,0:T(8,128)(2,1)S(1)} %slice.124), channel_id=1, source_target_pairs={{0,4},{4,8},{8,12},{1,5},{5,9},{9,13},{2,6},{6,10},{10,14},{3,7},{... | collective-permute-start | bytes 1572872 | tf_op jit(solution)/shard_map/ppermute | solution.py:25
  26.9 1.0 copy-start.6
  70.8 17.7 %copy-start.3 = (bf16[16,4,16,8,64]{4,3,2,1,0:T(8,128)(2,1)S(1)}, bf16[16,4,16,8,64]{4,3,2,1,0:T(8,128)(2,1)}, u32[]{:S(2)}) copy-start(bf16[16,4,16,8,64]{4,3,2,1,0:T(8,128)(2,1)} %reshape.84) | copy-start | bytes 3145732
  92.9 18.2 %copy-start.7 = (bf16[512,512]{1,0:T(8,128)(2,1)S(1)}, bf16[512,512]{1,0:T(8,128)(2,1)}, u32[]{:S(2)}) copy-start(bf16[512,512]{1,0:T(8,128)(2,1)} %param.10) | copy-start | bytes 1572868
  111.1 1.7 %copy-start.1 = (bf16[512,1536]{1,0:T(8,128)(2,1)S(1)}, bf16[512,1536]{1,0:T(8,128)(2,1)}, u32[]{:S(2)}) copy-start(bf16[512,1536]{1,0:T(8,128)(2,1)} %param.9) | copy-start | bytes 4718596
where the time goes:
time: 113 us
  blocking collectives  42.7 us (38%)
  matrix products  20.3 us (18%)
  other arithmetic  19 us (17%)
  local copies, waits for them, and re-layouts  15.9 us (14%)
  starting transfers between devices  7.72 us (7%)
  waiting for transfers between devices  6.9 us (6%)
    all_to_all x1, blocking collectives, per_device(): lax.all_to_all(normed, 'ta', split_axis=2, concat_axis=0, tiled=True)  24.7 us
    all_to_all x1, blocking collectives, attend_back(): return lax.all_to_all(output, 'ta', split_axis=0, concat_axis=2, tiled=True)  18 us
    sub x1, other arithmetic, attend(): expo = jnp.exp(scores - peak)  17.7 us
    dot_general x9, matrix products, conv_space(): jnp.dot(window.reshape(-1, channels), w_space[row_off, col_off], preferre...  8.59 us
    ppermute x1, starting transfers between devices, padded_2(): lax.ppermute(lax.slice_in_dim(block, block.shape[dim] - width, None, axis...  4.97 us
    ppermute x1, waiting for transfers between devices, padded_2(): lax.ppermute(lax.slice_in_dim(block, 0, width, axis=dim), axis, backward)  4.27 us
    dot_general x1, matrix products, attend(): jnp.einsum('frwhd,grwhd->rwhfg', queries.reshape(shape), keyset.reshape(s...  4.11 us
    reshape x1, local copies, waits for them, and re-layouts, attend(): queries.reshape(shape)  3.9 us
  transfers between devices with their start and end apart: 3, of which 3 were waited for; matrix products, arithmetic and copies ran while one was open for 3% of the time, Pallas kernels for 0%

commit v1 on v0

v1 whole, which is shorter than its diff:
```python
import functools

import jax
import jax.numpy as jnp
from jax import lax
from jax.experimental import pallas as pl
from jax.experimental.pallas import tpu as pltpu
from jax.sharding import PartitionSpec as P

HEADS = 8
LANE_TILE = 256
F32 = jnp.float32
BF16 = jnp.bfloat16


def padded_2(block, sides, width):
    for axis, dim in sides:
        count = lax.axis_size(axis)
        forward = [(i, i + 1) for i in range(count - 1)]
        backward = [(target, source) for source, target in forward]
        low = lax.ppermute(
            lax.slice_in_dim(block, block.shape[dim] - width, None, axis=dim), axis, forward
        )
        high = lax.ppermute(lax.slice_in_dim(block, 0, width, axis=dim), axis, backward)
        block = jnp.concatenate([low, block, high], axis=dim)
    return block


def from_behind(array, axis, by):
    devices = lax.axis_size(axis)
    pairs = [(i, i + by) for i in range(devices) if 0 <= i + by < devices]
    return lax.ppermute(array, axis, pairs)


def conv_space(padded, w_space, height, width):
    channels = padded.shape[-1]
    total = jnp.zeros(padded.shape[:1] + (height, width, channels), F32)
    for row_off in range(3):
        for col_off in range(3):
            window = padded[:, row_off : row_off + height, col_off : col_off + width, :]
            product = jnp.dot(
                window.reshape(-1, channels),
                w_space[row_off, col_off],
                preferred_element_type=F32,
            )
            total = total + product.reshape(total.shape)
    return total


def temporal_mix(clip, hidden, earlier, w_time, norm_gain):
    channels = clip.shape[-1]
    frames = hidden.shape[0]
    joined = jnp.concatenate([earlier, hidden], axis=0)
    total = jnp.zeros(hidden.shape, F32)
    for tap_index in range(3):
        window = joined[2 - tap_index : 2 - tap_index + frames]
        product = jnp.dot(
            window.reshape(-1, channels), w_time[tap_index], preferred_element_type=F32
        )
        total = total + product.reshape(hidden.shape)
    mixed = (clip.astype(F32) + total).astype(BF16)
    wide = mixed.astype(F32)
    scale = lax.rsqrt(jnp.mean(wide * wide, axis=-1, keepdims=True) + 1e-06)
    normed = (wide * scale * norm_gain).astype(BF16)
    return (mixed, normed)


def project(normed, w_qkv):
    channels = normed.shape[-1]
    flattened = jnp.dot(
        normed.reshape(-1, channels), w_qkv, preferred_element_type=F32
    ).astype(BF16)
    joined = flattened.reshape(normed.shape[:-1] + (3 * channels,))
    return (
        joined[..., :channels],
        joined[..., channels : 2 * channels],
        joined[..., 2 * channels :],
    )


def attend(queries, keyset, valueset, heads):
    frames, rows, cols, channels = queries.shape
    head_dim = channels // heads
    shape = (frames, rows, cols, heads, head_dim)
    scores = jnp.einsum(
        "frwhd,grwhd->rwhfg",
        queries.reshape(shape),
        keyset.reshape(shape),
        preferred_element_type=F32,
    )
    scores = scores * (1.0 / head_dim**0.5)
    peak = jnp.max(scores, axis=-1, keepdims=True)
    expo = jnp.exp(scores - peak)
    probs = (expo / jnp.sum(expo, axis=-1, keepdims=True)).astype(BF16)
    output = jnp.einsum(
        "rwhfg,grwhd->frwhd", probs, valueset.reshape(shape), preferred_element_type=F32
    )
    return output.reshape(queries.shape).astype(BF16)


def plain_device(clip, w_space, w_time, w_qkv, w_out, norm_gain):
    frames, height, width, channels = clip.shape
    rimmed = padded_2(clip, (("gy", 1),), 1)
    padded = jnp.pad(rimmed, ((0, 0), (0, 0), (1, 1), (0, 0)))
    hidden = jax.nn.silu(conv_space(padded, w_space, height, width)).astype(BF16)
    earlier = from_behind(hidden[-2:], "ta", 1)
    mixed, normed = temporal_mix(clip, hidden, earlier, w_time, norm_gain)
    queries, keyset, valueset = project(
        lax.all_to_all(normed, "ta", split_axis=2, concat_axis=0, tiled=True), w_qkv
    )
    output = attend(queries, keyset, valueset, HEADS)
    attended = lax.all_to_all(output, "ta", split_axis=0, concat_axis=2, tiled=True)
    projected = jnp.dot(
        attended.reshape(-1, channels), w_out, preferred_element_type=F32
    ).reshape(clip.shape)
    return (mixed.astype(F32) + projected).astype(BF16)


def pack_kernel(n, me_ref, clip_ref, *outs):
    frames, height, width, channels = clip_ref.shape
    cw = width // n
    edge, mid = outs[:n], outs[n:]
    me = me_ref[0]
    iota = lax.broadcasted_iota(jnp.int32, (2 * frames, channels), 0)
    order = [0, height - 1] + list(range(1, height - 1))
    for m in range(n):
        g = me ^ m
        here = pl.multiple_of(g * cw, cw)
        before = pl.multiple_of(jnp.maximum(g - 1, 0) * cw, cw)
        after = pl.multiple_of(jnp.minimum(g + 1, n - 1) * cw, cw)
        has_left = g > 0
        has_right = g < n - 1
        for slot, r in enumerate(order):
            dst = edge[m] if slot < 2 else mid[m]
            at = slot if slot < 2 else slot - 2
            rim = jnp.zeros((2 * frames, channels), F32)
            for f in range(frames):
                dst[at, f * cw : (f + 1) * cw, :] = clip_ref[f, r, pl.ds(here, cw), :]
                left = clip_ref[f, r, pl.ds(before, cw), :].astype(F32)[cw - 1 : cw, :]
                right = clip_ref[f, r, pl.ds(after, cw), :].astype(F32)[0:1, :]
                rim = jnp.where((iota == f) & has_left, left, rim)
                rim = jnp.where((iota == frames + f) & has_right, right, rim)
            dst[at, frames * cw : frames * (cw + 2), :] = rim.astype(BF16)


def pack(clip, me, n):
    frames, height, width, channels = clip.shape
    cw = width // n
    piece = frames * (cw + 2)
    shapes = [jax.ShapeDtypeStruct((2, piece, channels), BF16)] * n
    shapes += [jax.ShapeDtypeStruct((height - 2, piece, channels), BF16)] * n
    vm = pl.BlockSpec(memory_space=pltpu.VMEM)
    outs = pl.pallas_call(
        functools.partial(pack_kernel, n),
        out_shape=shapes,
        in_specs=[pl.BlockSpec(memory_space=pltpu.SMEM), vm],
        out_specs=[vm] * (2 * n),
        name="pack",
        compiler_params=pltpu.CompilerParams(vmem_limit_bytes=12 * 2**20),
        cost_estimate=pl.CostEstimate(flops=10**7, bytes_accessed=3 * clip.size * 2, transcendentals=0),
    )(me, clip)
    return outs[:n], outs[n:]


def main_kernel(n, frames, plan, n_edge, n_mid, has_z, *refs):
    refs = list(refs)
    me_ref = refs.pop(0)
    edge = [refs.pop(0) for _ in range(n)]
    mid = [refs.pop(0) for _ in range(n)]
    zs = [refs.pop(0) for _ in range(2)] if has_z else []
    ws_ref, wt_ref, wqkv_ref, wo_ref, gain_ref = [refs.pop(0) for _ in range(5)]
    outs = [refs.pop(0) for _ in range(n)]
    xs, hs, hb, tt, nb, mx, qkv, at, of, bias, ones = refs
    channels = gain_ref.shape[-1]
    total = n * frames
    cw = xs.shape[3]
    halves = cw // 8
    rows = len(plan)
    block = total * 8
    tokens = rows * halves * block
    nt = channels // LANE_TILE
    me = me_ref[0]

    iota = lax.broadcasted_iota(jnp.int32, (cw, channels), 0)
    for slot, (kind, index) in enumerate(sum(plan, ())):
        for m in range(n):
            base = (me ^ m) * frames
            if kind == "z":
                src = zs[index].at[m]
            else:
                src = (edge if kind == "e" else mid)[m].at[index]
            rim = src[frames * cw : frames * (cw + 2), :].astype(F32)
            for f in range(frames):
                here = src[f * cw : (f + 1) * cw, :]
                wide = here.astype(F32)
                left = jnp.where(iota == 0, rim[f : f + 1, :], pltpu.roll(wide, 1, 0))
                right = jnp.where(
                    iota == cw - 1, rim[frames + f : frames + f + 1, :], pltpu.roll(wide, cw - 1, 0)
                )
                xs[slot, 0, base + f] = left.astype(BF16)
                xs[slot, 1, base + f] = here
                xs[slot, 2, base + f] = right.astype(BF16)

    for i in range(rows):
        for ch in range(halves):
            hs[i, ch, 0:2] = jnp.zeros((2, 8, channels), F32)

    def conv_step(t, carry):
        i, j = t // nt, t % nt
        cols = pl.ds(pl.multiple_of(j * LANE_TILE, LANE_TILE), LANE_TILE)
        acc = jnp.zeros((total * cw, LANE_TILE), F32)
        for a in range(3):
            for b in range(3):
                lhs = xs[3 * i + a, b].reshape(total * cw, channels)
                acc = acc + jnp.dot(lhs, ws_ref[a, b, :, cols], preferred_element_type=F32)
        hidden = (acc * jax.nn.sigmoid(acc)).reshape(total, halves, 8, LANE_TILE)
        for ch in range(halves):
            hs[i, ch, 2:, :, cols] = hidden[:, ch]
        return carry

    lax.fori_loop(0, rows * nt, conv_step, 0)

    for k in range(3):
        for i in range(rows):
            for ch in range(halves):
                first = (i * halves + ch) * block
                hb[k, first : first + block, :] = (
                    hs[i, ch, 2 - k : 2 - k + total].reshape(block, channels).astype(BF16)
                )
    per_row = halves * block

    def time_step(t, carry):
        i, j = t // nt, t % nt
        cols = pl.ds(pl.multiple_of(j * LANE_TILE, LANE_TILE), LANE_TILE)
        span = pl.ds(pl.multiple_of(i * per_row, per_row), per_row)
        acc = jnp.zeros((per_row, LANE_TILE), F32)
        for k in range(3):
            acc = acc + jnp.dot(hb[k, span, :], wt_ref[k, :, cols], preferred_element_type=F32)
        tt[span, cols] = acc
        return carry

    lax.fori_loop(0, rows * nt, time_step, 0)

    gain = gain_ref[...]

    def norm_step(i, carry):
        clip = xs[3 * i + 1, 1].astype(F32).reshape(total, halves, 8, channels)
        for ch in range(halves):
            span = pl.ds(pl.multiple_of((i * halves + ch) * block, block), block)
            mixed = (clip[:, ch].reshape(block, channels) + tt[span, :]).astype(BF16)
            wide = mixed.astype(F32)
            scale = lax.rsqrt(jnp.mean(wide * wide, axis=-1, keepdims=True) + 1e-06)
            mx[span, :] = mixed
            nb[span, :] = (wide * scale * gain).astype(BF16)
        return carry

    lax.fori_loop(0, rows, norm_step, 0)

    head_dim = channels // HEADS
    root = 1.0 / head_dim**0.5

    def qkv_step(t, carry):
        i, j = t // (3 * nt), t % (3 * nt)
        cols = pl.ds(pl.multiple_of(j * LANE_TILE, LANE_TILE), LANE_TILE)
        span = pl.ds(pl.multiple_of(i * per_row, per_row), per_row)
        product = jnp.dot(nb[span, :], wqkv_ref[:, cols], preferred_element_type=F32)
        qkv[span, cols] = product.astype(BF16)
        return carry

    lax.fori_loop(0, rows * 3 * nt, qkv_step, 0)

    pair = 2 * head_dim
    ri = lax.broadcasted_iota(jnp.int32, (block, 2 * block), 0) % 8
    ci = lax.broadcasted_iota(jnp.int32, (block, 2 * block), 1) % 8
    bias[...] = jnp.where(ri == ci, 0.0, -1e30).astype(F32)
    oi = lax.broadcasted_iota(jnp.int32, (2 * block, pair), 0) // block
    ol = lax.broadcasted_iota(jnp.int32, (2 * block, pair), 1) // head_dim
    ones[...] = jnp.where(oi == ol, 1.0, 0.0).astype(BF16)

    def attend_step(b, carry):
        span = pl.ds(pl.multiple_of(b * block, block), block)
        low = lax.broadcasted_iota(jnp.int32, (block, pair), 1) < head_dim
        zero = jnp.zeros((block, pair), BF16)
        for p in range(channels // pair):
            q = qkv[span, p * pair : (p + 1) * pair] * jnp.asarray(root, BF16)
            k = qkv[span, channels + p * pair : channels + (p + 1) * pair]
            v = qkv[span, 2 * channels + p * pair : 2 * channels + (p + 1) * pair]
            keys = jnp.concatenate([jnp.where(low, k, zero), jnp.where(low, zero, k)], axis=0)
            vals = jnp.concatenate([jnp.where(low, v, zero), jnp.where(low, zero, v)], axis=0)
            s = lax.dot_general(q, keys, (((1,), (1,)), ((), ())), preferred_element_type=F32)
            s = s + bias[...]
            s0, s1 = s[:, :block], s[:, block:]
            e0 = jnp.exp(s0 - jnp.max(s0, axis=-1, keepdims=True)).astype(BF16)
            e1 = jnp.exp(s1 - jnp.max(s1, axis=-1, keepdims=True)).astype(BF16)
            probs = jnp.concatenate([e0, e1], axis=1)
            rhs = jnp.concatenate([vals, ones[...]], axis=1)
            o = jnp.dot(probs, rhs, preferred_element_type=F32)
            at[span, p * pair : (p + 1) * pair] = (o[:, :pair] / o[:, pair:]).astype(BF16)
        return carry

    lax.fori_loop(0, rows * halves, attend_step, 0)

    def out_step(t, carry):
        i, j = t // nt, t % nt
        cols = pl.ds(pl.multiple_of(j * LANE_TILE, LANE_TILE), LANE_TILE)
        span = pl.ds(pl.multiple_of(i * per_row, per_row), per_row)
        product = jnp.dot(at[span, :], wo_ref[:, cols], preferred_element_type=F32)
        result = (mx[span, cols].astype(F32) + product).reshape(halves, total, 8, LANE_TILE)
        of[i, :, :, :, cols] = result
        return carry

    lax.fori_loop(0, rows * nt, out_step, 0)
    for m in range(n):
        base = (me ^ m) * frames
        for i in range(rows):
            parts = [of[i, ch, pl.ds(base, frames)] for ch in range(halves)]
            outs[m][i] = jnp.concatenate(parts, axis=1).astype(BF16)


def main(me, edge, mid, zs, weights, plan, frames, cw, name):
    n = len(edge)
    w_space, w_time, w_qkv, w_out, norm_gain = weights
    channels = w_out.shape[0]
    total = n * frames
    rows = len(plan)
    halves = cw // 8
    block = total * 8
    tokens = rows * halves * block
    vm = pl.BlockSpec(memory_space=pltpu.VMEM)
    n_in = 2 * n + len(zs) + 5
    return pl.pallas_call(
        functools.partial(main_kernel, n, frames, plan, 2, mid[0].shape[0], bool(zs)),
        out_shape=[jax.ShapeDtypeStruct((rows, frames, cw, channels), BF16)] * n,
        in_specs=[pl.BlockSpec(memory_space=pltpu.SMEM)] + [vm] * n_in,
        out_specs=[vm] * n,
        scratch_shapes=[
            pltpu.VMEM((3 * rows, 3, total, cw, channels), BF16),
            pltpu.VMEM((rows, halves, total + 2, 8, channels), F32),
            pltpu.VMEM((3, tokens, channels), BF16),
            pltpu.VMEM((tokens, channels), F32),
            pltpu.VMEM((tokens, channels), BF16),
            pltpu.VMEM((tokens, channels), BF16),
            pltpu.VMEM((tokens, 3 * channels), BF16),
            pltpu.VMEM((tokens, channels), BF16),
            pltpu.VMEM((rows, halves, total, 8, channels), F32),
            pltpu.VMEM((block, 2 * block), F32),
            pltpu.VMEM((2 * block, 2 * channels // HEADS), BF16),
        ],
        name=name,
        compiler_params=pltpu.CompilerParams(vmem_limit_bytes=32 * 2**20),
        cost_estimate=pl.CostEstimate(
            flops=2 * tokens * channels * channels * 16, bytes_accessed=10**6, transcendentals=tokens * channels
        ),
    )(me, *edge, *mid, *zs, w_space, w_time, w_qkv, w_out, norm_gain.reshape(1, channels))


def join_kernel(n, me_ref, *refs):
    outer, inner, out_ref = refs[:n], refs[n : 2 * n], refs[2 * n]
    frames, height, width, channels = out_ref.shape
    cw = width // n
    me = me_ref[0]
    order = [0, height - 1] + list(range(1, height - 1))
    for m in range(n):
        at = pl.ds(pl.multiple_of((me ^ m) * cw, cw), cw)
        for slot, r in enumerate(order):
            src = outer[m].at[slot] if slot < 2 else inner[m].at[slot - 2]
            for f in range(frames):
                out_ref[f, r, at, :] = src[f]


def join(me, outer, inner, shape):
    n = len(outer)
    vm = pl.BlockSpec(memory_space=pltpu.VMEM)
    return pl.pallas_call(
        functools.partial(join_kernel, n),
        out_shape=jax.ShapeDtypeStruct(shape, BF16),
        in_specs=[pl.BlockSpec(memory_space=pltpu.SMEM)] + [vm] * (2 * n),
        out_specs=vm,
        name="join",
        compiler_params=pltpu.CompilerParams(vmem_limit_bytes=12 * 2**20),
    )(me, *outer, *inner)


def kernel_device(clip, w_space, w_time, w_qkv, w_out, norm_gain):
    frames, height, width, channels = clip.shape
    n = lax.axis_size("ta")
    cw = width // n
    me = lax.axis_index("ta").astype(jnp.int32).reshape(1)
    weights = (w_space, w_time, w_qkv, w_out, norm_gain)

    def swap(pieces):
        return [pieces[0]] + [
            lax.ppermute(pieces[m], "ta", [(i, i ^ m) for i in range(n)]) for m in range(1, n)
        ]

    edge, mid = pack(clip, me, n)
    edge = swap(edge)
    mid = swap(mid)
    count = lax.axis_size("gy")
    forward = [(i, i + 1) for i in range(count - 1)]
    backward = [(b, a) for a, b in forward]
    above = lax.ppermute(jnp.stack([e[1] for e in edge]), "gy", forward)
    below = lax.ppermute(jnp.stack([e[0] for e in edge]), "gy", backward)

    def where(r):
        if r < 0:
            return ("z", 0)
        if r >= height:
            return ("z", 1)
        if r == 0:
            return ("e", 0)
        if r == height - 1:
            return ("e", 1)
        return ("m", r - 1)

    def plan(rows):
        return tuple(tuple(where(r + a - 1) for a in range(3)) for r in rows)

    inner = main(me, edge, mid, [], weights, plan(range(1, height - 1)), frames, cw, "inner")
    inner = swap(inner)
    outer = main(me, edge, mid, [above, below], weights, plan([0, height - 1]), frames, cw, "outer")
    outer = swap(outer)
    return join(me, outer, inner, clip.shape)


def solution(mesh):
    n = mesh.shape["ta"]
    rows_axis = mesh.shape["gy"]

    def per_device(clip, w_space, w_time, w_qkv, w_out, norm_gain):
        frames, height, width, channels = clip.shape
        tiled = (
            n & (n - 1) == 0
            and width % n == 0
            and (width // n) % 16 == 0
            and (2 * frames) % 8 == 0
            and frames * n * 8 == 128
            and height >= 3
            and channels % LANE_TILE == 0
            and 2 * channels // HEADS == 128
        )
        device = kernel_device if tiled else plain_device
        return device(clip, w_space, w_time, w_qkv, w_out, norm_gain)

    in_specs = (P(("ga", "ta"), "gy", None, None), P(), P(), P(), P(), P())
    out_specs = P(("ga", "ta"), "gy", None, None)
    return jax.shard_map(
        per_device, mesh=mesh, in_specs=in_specs, out_specs=out_specs, check_vma=False
    )
```

time: 113 us -> 56.9 us (0.50)
  blocking collectives: 42.7 us -> 0 us
  Pallas kernels: 0 us -> 25.1 us
  matrix products: 20.3 us -> 0 us
  other arithmetic: 19 us -> 0.08 us
  local copies, waits for them, and re-layouts: 15.9 us -> 4.66 us
  starting transfers between devices: 7.72 us -> 14.2 us
  waiting for transfers between devices: 6.9 us -> 12.2 us
    all_to_all x2 -> x0, blocking collectives: 42.7 us -> none  [the longest x1 24.7 us: per_device(): lax.all_to_all(normed, 'ta', split_axis=2, concat_axis=0, tiled=True)]
    pallas_call x0 -> x4, Pallas kernels: none -> 25.1 us  [the longest x2 23.9 us: main(): pl.pallas_call(functools.partial(main_kernel, n, frames, plan, 2, mid[0]....]
    dot_general x16 -> x0, matrix products: 20.3 us -> none  [the longest x9 8.59 us: conv_space(): jnp.dot(window.reshape(-1, channels), w_space[row_off, col_off], preferre...]
    sub x1 -> x0, other arithmetic: 17.7 us -> none  [attend(): expo = jnp.exp(scores - peak)]
    reshape x3 -> x0, local copies, waits for them, and re-layouts: 8.8 us -> none  [the longest x1 3.9 us: attend(): queries.reshape(shape)]
    ppermute x3 -> x14, starting transfers between devices: 7.72 us -> 14.2 us  [the longest x12 9.46 us: swap(): lax.ppermute(pieces[m], 'ta', [(i, i ^ m) for i in range(n)])]
    ppermute x3 -> x14, waiting for transfers between devices: 6.9 us -> 12.2 us  [the longest x12 12.2 us: swap(): lax.ppermute(pieces[m], 'ta', [(i, i ^ m) for i in range(n)])]
    unnamed x16, local copies, waits for them, and re-layouts: 0.04 us -> 4.62 us
  transfers between devices with their start and end apart: 3 -> 14, of which waited for: 3 -> 5; matrix products, arithmetic and copies ran while one was open for 3% -> 0% of each run, Pallas kernels for 0% -> 42%
where the time goes in v1:
time: 56.9 us; the launch traced here: 56.5 us
  Pallas kernels  25.1 us (44%)
  starting transfers between devices  14.2 us (25%)
  waiting for transfers between devices  12.2 us (21%)
  local copies, waits for them, and re-layouts  4.66 us (8%)
    pallas_call x2, Pallas kernels, main(): pl.pallas_call(functools.partial(main_kernel, n, frames, plan, 2, mid[0]....  23.9 us
    ppermute x12, waiting for transfers between devices, swap(): lax.ppermute(pieces[m], 'ta', [(i, i ^ m) for i in range(n)])  12.2 us
    ppermute x12, starting transfers between devices, swap(): lax.ppermute(pieces[m], 'ta', [(i, i ^ m) for i in range(n)])  9.46 us
    unnamed x16, local copies, waits for them, and re-layouts  4.62 us
    ppermute x1, starting transfers between devices, kernel_device(): above = lax.ppermute(jnp.stack([e[1] for e in edge]), 'gy', forward)  3.5 us
    ppermute x1, starting transfers between devices, kernel_device(): below = lax.ppermute(jnp.stack([e[0] for e in edge]), 'gy', backward)  1.29 us
  transfers between devices with their start and end apart: 14, of which 5 were waited for; matrix products, arithmetic and copies ran while one was open for 0% of the time, Pallas kernels for 42%

profile of v1, /device:TPU:0, one launch (start us, length us, event | category | flops | bytes accessed | tf_op | source)
XLA Modules:
  0.0 56.5 jit_solution(9148012035286265190)
XLA Ops:
  0.0 0.0 copy-start
  0.0 1.2 %copy-done = bf16[4,4,64,512]{3,2,1,0:T(8,128)(2,1)S(1)} copy-done((bf16[4,4,64,512]{3,2,1,0:T(8,128)(2,1)S(1)}, bf16[4,4,64,512]{3,2,1,0:T(8,128)(2,1)}, u32[]{:S(2)}) %copy-start) | copy-done | bytes 1048600
  1.2 0.0 copy-start.3
  1.2 0.0 copy-start.4
  1.2 0.0 copy-start.7
  1.2 0.2 pack.1
  1.5 0.6 collective-permute-start
  2.0 2.6 %collective-permute-start.1 = (bf16[2,72,512]{2,1,0:T(8,128)(2,1)S(1)}, bf16[2,72,512]{2,1,0:T(8,128)(2,1)S(1)}, u32[]{:S(2)}, u32[]{:S(2)}) collective-permute-start(bf16[2,72,512]{2,1,0:T(8,128)(2,1)S(1)} %get-tuple-element.23), channel_id=1, source_target_pairs={{0,8},{4,12},{8,0},{12,4},{1,9},{5,13},{9,1},{13,5},{2,10},{6,14},... | collective-permute-start | bytes 442376 | tf_op jit(solution)/shard_map/ppermute | solution.py:393
  4.6 0.0 collective-permute-start.2
  4.6 0.2 collective-permute-start.3
  4.8 1.9 %collective-permute-start.4 = (bf16[2,72,512]{2,1,0:T(8,128)(2,1)S(1)}, bf16[2,72,512]{2,1,0:T(8,128)(2,1)S(1)}, u32[]{:S(2)}, u32[]{:S(2)}) collective-permute-start(bf16[2,72,512]{2,1,0:T(8,128)(2,1)S(1)} %get-tuple-element.27), channel_id=1, source_target_pairs={{0,8},{4,12},{8,0},{12,4},{1,9},{5,13},{9,1},{13,5},{2,10},{6,14},... | collective-permute-start | bytes 442376 | tf_op jit(solution)/shard_map/ppermute | solution.py:393
  6.8 0.0 collective-permute-done.refs_2_
  6.8 0.1 collective-permute-start.5
  6.9 2.4 %collective-permute-done.1.refs_3_ = bf16[2,72,512]{2,1,0:T(8,128)(2,1)S(1)} collective-permute-done((bf16[2,72,512]{2,1,0:T(8,128)(2,1)S(1)}, bf16[2,72,512]{2,1,0:T(8,128)(2,1)S(1)}, u32[]{:S(2)}, u32[]{:S(2)}) %collective-permute-start.1) | collective-permute-done | bytes 147488 | tf_op jit(solution)/shard_map/ppermute | solution.py:393
  9.3 2.7 %collective-permute-done.2.refs_4_ = bf16[2,72,512]{2,1,0:T(8,128)(2,1)S(1)} collective-permute-done((bf16[2,72,512]{2,1,0:T(8,128)(2,1)S(1)}, bf16[2,72,512]{2,1,0:T(8,128)(2,1)S(1)}, u32[]{:S(2)}, u32[]{:S(2)}) %collective-permute-start.2) | collective-permute-done | bytes 147488 | tf_op jit(solution)/shard_map/ppermute | solution.py:393
  12.1 3.5 %collective-permute-start.6 = (bf16[4,72,512]{2,1,0:T(8,128)(2,1)S(1)}, bf16[4,72,512]{2,1,0:T(8,128)(2,1)S(1)}, u32[]{:S(2)}, u32[]{:S(2)}) collective-permute-start(bf16[4,72,512]{2,1,0:T(8,128)(2,1)S(1)} %pad_maximum_fusion), channel_id=1, source_target_pairs={{0,1},{1,2},{2,3},{4,5},{5,6},{6,7},{8,9},{9,10},{10,11},{12,13},{... | collective-permute-start | bytes 884744 | tf_op jit(solution)/shard_map/ppermute | solution.py:402
  15.6 1.3 %collective-permute-start.7 = (bf16[4,72,512]{2,1,0:T(8,128)(2,1)S(1)}, bf16[4,72,512]{2,1,0:T(8,128)(2,1)S(1)}, u32[]{:S(2)}, u32[]{:S(2)}) collective-permute-start(bf16[4,72,512]{2,1,0:T(8,128)(2,1)S(1)} %pad_maximum_fusion.1), channel_id=1, source_target_pairs={{1,0},{2,1},{3,2},{5,4},{6,5},{7,6},{9,8},{10,9},{11,10},{13,12},{... | collective-permute-start | bytes 884744 | tf_op jit(solution)/shard_map/ppermute | solution.py:403
  16.9 0.0 collective-permute-done.3.refs_6_
  16.9 0.0 collective-permute-done.4.refs_7_
  16.9 1.3 %collective-permute-done.5.refs_8_ = bf16[2,72,512]{2,1,0:T(8,128)(2,1)S(1)} collective-permute-done((bf16[2,72,512]{2,1,0:T(8,128)(2,1)S(1)}, bf16[2,72,512]{2,1,0:T(8,128)(2,1)S(1)}, u32[]{:S(2)}, u32[]{:S(2)}) %collective-permute-start.5) | collective-permute-done | bytes 147488 | tf_op jit(solution)/shard_map/ppermute | solution.py:393
  18.3 0.0 copy-done.3
  18.3 0.0 copy-done.4
  18.3 0.0 copy-done.7
  18.3 0.0 copy-start.1
  18.3 2.3 %copy-done.1 = bf16[3,3,512,512]{3,2,1,0:T(8,128)(2,1)S(1)} copy-done((bf16[3,3,512,512]{3,2,1,0:T(8,128)(2,1)S(1)}, bf16[3,3,512,512]{3,2,1,0:T(8,128)(2,1)}, u32[]{:S(2)}) %copy-start.1) | copy-done | bytes 4718616
  20.6 0.0 copy-start.5
  20.6 1.0 %copy-done.5 = bf16[512,512]{1,0:T(8,128)(2,1)S(1)} copy-done((bf16[512,512]{1,0:T(8,128)(2,1)S(1)}, bf16[512,512]{1,0:T(8,128)(2,1)}, u32[]{:S(2)}) %copy-start.5) | copy-done | bytes 524312
  21.6 0.0 copy-start.2
  21.7 0.0 copy-start.6
  21.7 11.9 %inner.1 = (bf16[2,4,16,512]{3,2,1,0:T(8,128)(2,1)S(1)}, bf16[2,4,16,512]{3,2,1,0:T(8,128)(2,1)S(1)}, bf16[2,4,16,512]{3,2,1,0:T(8,128)(2,1)S(1)}, bf16[2,4,16,512]{3,2,1,0:T(8,128)(2,1)S(1)}) custom-call(s32[1]{0:T(128)} %bitcast.me_ref.refs_0_, bf16[2,72,512]{2,1,0:T(8,128)(2,1)S(1)} %get-tuple-element.21.refs_1_, ...), custom_call_target="tpu_custom_call" | custom-call | flops 4294967296 | bytes 1000000 | tf_op jit(solution)/shard_map/inner/pallas_call | solution.py:331
  33.6 0.2 collective-permute-start.11
  33.8 1.7 %collective-permute-start.12 = (bf16[2,4,16,512]{3,2,1,0:T(8,128)(2,1)S(1)}, bf16[2,4,16,512]{3,2,1,0:T(8,128)(2,1)S(1)}, u32[]{:S(2)}, u32[]{:S(2)}) collective-permute-start(bf16[2,4,16,512]{3,2,1,0:T(8,128)(2,1)S(1)} %get-tuple-element.35), channel_id=1, source_target_pairs={{0,8},{4,12},{8,0},{12,4},{1,9},{5,13},{9,1},{13,5},{2,10},{6,14},... | collective-permute-start | bytes 393224 | tf_op jit(solution)/shard_map/ppermute | solution.py:393
  35.5 0.0 collective-permute-start.13
  35.5 0.0 collective-permute-done.6.refs_9_
  35.5 0.0 collective-permute-done.7.refs_10_
  35.5 0.0 copy-done.2
  35.5 0.0 copy-done.6
  35.5 11.9 %outer.1 = (bf16[2,4,16,512]{3,2,1,0:T(8,128)(2,1)S(1)}, bf16[2,4,16,512]{3,2,1,0:T(8,128)(2,1)S(1)}, bf16[2,4,16,512]{3,2,1,0:T(8,128)(2,1)S(1)}, bf16[2,4,16,512]{3,2,1,0:T(8,128)(2,1)S(1)}) custom-call(s32[1]{0:T(128)} %bitcast.me_ref.refs_0_, bf16[2,72,512]{2,1,0:T(8,128)(2,1)S(1)} %get-tuple-element.21.refs_1_, ...), custom_call_target="tpu_custom_call" | custom-call | flops 4294967296 | bytes 1000000 | tf_op jit(solution)/shard_map/outer/pallas_call | solution.py:331
  47.5 0.5 collective-permute-start.8
  47.9 1.7 %collective-permute-start.9 = (bf16[2,4,16,512]{3,2,1,0:T(8,128)(2,1)S(1)}, bf16[2,4,16,512]{3,2,1,0:T(8,128)(2,1)S(1)}, u32[]{:S(2)}, u32[]{:S(2)}) collective-permute-start(bf16[2,4,16,512]{3,2,1,0:T(8,128)(2,1)S(1)} %get-tuple-element.31), channel_id=1, source_target_pairs={{0,8},{4,12},{8,0},{12,4},{1,9},{5,13},{9,1},{13,5},{2,10},{6,14},... | collective-permute-start | bytes 393224 | tf_op jit(solution)/shard_map/ppermute | solution.py:393
  49.6 0.0 collective-permute-done.11.refs_5_
  49.7 0.0 collective-permute-start.10
  49.7 0.0 collective-permute-done.12.refs_6_
  49.7 0.0 collective-permute-done.13.refs_7_
  49.7 0.0 collective-permute-done.8.refs_1_
  49.7 4.6 %collective-permute-done.9.refs_2_ = bf16[2,4,16,512]{3,2,1,0:T(8,128)(2,1)S(1)} collective-permute-done((bf16[2,4,16,512]{3,2,1,0:T(8,128)(2,1)S(1)}, bf16[2,4,16,512]{3,2,1,0:T(8,128)(2,1)S(1)}, u32[]{:S(2)}, u32[]{:S(2)}) %collective-permute-start.9) | collective-permute-done | bytes 131104 | tf_op jit(solution)/shard_map/ppermute | solution.py:393
  54.3 1.2 %collective-permute-done.10.refs_3_ = bf16[2,4,16,512]{3,2,1,0:T(8,128)(2,1)S(1)} collective-permute-done((bf16[2,4,16,512]{3,2,1,0:T(8,128)(2,1)S(1)}, bf16[2,4,16,512]{3,2,1,0:T(8,128)(2,1)S(1)}, u32[]{:S(2)}, u32[]{:S(2)}) %collective-permute-start.10) | collective-permute-done | bytes 131104 | tf_op jit(solution)/shard_map/ppermute | solution.py:393
  55.5 1.0 %join.1 = bf16[4,4,64,512]{3,2,1,0:T(8,128)(2,1)} custom-call(s32[1]{0:T(128)} %bitcast.me_ref.refs_0_, bf16[2,4,16,512]{3,2,1,0:T(8,128)(2,1)S(1)} %get-tuple-element.29.refs_0_, bf16[2,4,16,512]{3,2,1,0:T(8,128)(2,1)S(1)} %collective-permute-done.8.refs_1_, bf16[2,4,16,512]{3,2,1,0:T(8,128)(2,1)S(1)} %collective-permute-done.9.refs_2_, ...), custom_call_target="tpu_custom_call" | custom-call | tf_op jit(solution)/shard_map/join/pallas_call | solution.py:374
  (6 shorter events, 0.1 us)
Async XLA Ops:
  0.0 1.2 %copy-start = (bf16[4,4,64,512]{3,2,1,0:T(8,128)(2,1)S(1)}, bf16[4,4,64,512]{3,2,1,0:T(8,128)(2,1)}, u32[]{:S(2)}) copy-start(bf16[4,4,64,512]{3,2,1,0:T(8,128)(2,1)} %clip_ref.1) | copy-start | bytes 3145732
  1.2 17.0 %copy-start.3 = (bf16[3,512,512]{2,1,0:T(8,128)(2,1)S(1)}, bf16[3,512,512]{2,1,0:T(8,128)(2,1)}, u32[]{:S(2)}) copy-start(bf16[3,512,512]{2,1,0:T(8,128)(2,1)} %refs_10_.1) | copy-start | bytes 4718596
  1.2 17.0 %copy-start.4 = (bf16[512,1536]{1,0:T(8,128)(2,1)S(1)}, bf16[512,1536]{1,0:T(8,128)(2,1)}, u32[]{:S(2)}) copy-start(bf16[512,1536]{1,0:T(8,128)(2,1)} %refs_11_.3) | copy-start | bytes 4718596
  1.2 17.0 %copy-start.7 = (f32[512]{0:T(512)S(1)}, f32[512]{0:T(512)}, u32[]{:S(2)}) copy-start(f32[512]{0:T(512)} %param.11) | copy-start | bytes 6148
  1.5 5.3 %collective-permute-start = (bf16[2,72,512]{2,1,0:T(8,128)(2,1)S(1)}, bf16[2,72,512]{2,1,0:T(8,128)(2,1)S(1)}, u32[]{:S(2)}, u32[]{:S(2)}) collective-permute-start(bf16[2,72,512]{2,1,0:T(8,128)(2,1)S(1)} %get-tuple-element.22), channel_id=1, source_target_pairs={{0,4},{4,0},{8,12},{12,8},{1,5},{5,1},{9,13},{13,9},{2,6},{6,2},{1... | collective-permute-start | bytes 442376 | tf_op jit(solution)/shard_map/ppermute | solution.py:393
  2.0 7.3 %collective-permute-start.1 = (bf16[2,72,512]{2,1,0:T(8,128)(2,1)S(1)}, bf16[2,72,512]{2,1,0:T(8,128)(2,1)S(1)}, u32[]{:S(2)}, u32[]{:S(2)}) collective-permute-start(bf16[2,72,512]{2,1,0:T(8,128)(2,1)S(1)} %get-tuple-element.23), channel_id=1, source_target_pairs={{0,8},{4,12},{8,0},{12,4},{1,9},{5,13},{9,1},{13,5},{2,10},{6,14},... | collective-permute-start | bytes 442376 | tf_op jit(solution)/shard_map/ppermute | solution.py:393
  4.6 7.4 %collective-permute-start.2 = (bf16[2,72,512]{2,1,0:T(8,128)(2,1)S(1)}, bf16[2,72,512]{2,1,0:T(8,128)(2,1)S(1)}, u32[]{:S(2)}, u32[]{:S(2)}) collective-permute-start(bf16[2,72,512]{2,1,0:T(8,128)(2,1)S(1)} %get-tuple-element.24), channel_id=1, source_target_pairs={{0,12},{4,8},{8,4},{12,0},{1,13},{5,9},{9,5},{13,1},{2,14},{6,10},... | collective-permute-start | bytes 442376 | tf_op jit(solution)/shard_map/ppermute | solution.py:393
  4.6 12.3 %collective-permute-start.3 = (bf16[2,72,512]{2,1,0:T(8,128)(2,1)S(1)}, bf16[2,72,512]{2,1,0:T(8,128)(2,1)S(1)}, u32[]{:S(2)}, u32[]{:S(2)}) collective-permute-start(bf16[2,72,512]{2,1,0:T(8,128)(2,1)S(1)} %get-tuple-element.26), channel_id=1, source_target_pairs={{0,4},{4,0},{8,12},{12,8},{1,5},{5,1},{9,13},{13,9},{2,6},{6,2},{1... | collective-permute-start | bytes 442376 | tf_op jit(solution)/shard_map/ppermute | solution.py:393
  4.8 12.1 %collective-permute-start.4 = (bf16[2,72,512]{2,1,0:T(8,128)(2,1)S(1)}, bf16[2,72,512]{2,1,0:T(8,128)(2,1)S(1)}, u32[]{:S(2)}, u32[]{:S(2)}) collective-permute-start(bf16[2,72,512]{2,1,0:T(8,128)(2,1)S(1)} %get-tuple-element.27), channel_id=1, source_target_pairs={{0,8},{4,12},{8,0},{12,4},{1,9},{5,13},{9,1},{13,5},{2,10},{6,14},... | collective-permute-start | bytes 442376 | tf_op jit(solution)/shard_map/ppermute | solution.py:393
  6.8 11.5 %collective-permute-start.5 = (bf16[2,72,512]{2,1,0:T(8,128)(2,1)S(1)}, bf16[2,72,512]{2,1,0:T(8,128)(2,1)S(1)}, u32[]{:S(2)}, u32[]{:S(2)}) collective-permute-start(bf16[2,72,512]{2,1,0:T(8,128)(2,1)S(1)} %get-tuple-element.28), channel_id=1, source_target_pairs={{0,12},{4,8},{8,4},{12,0},{1,13},{5,9},{9,5},{13,1},{2,14},{6,10},... | collective-permute-start | bytes 442376 | tf_op jit(solution)/shard_map/ppermute | solution.py:393
  12.1 23.5 %collective-permute-start.6 = (bf16[4,72,512]{2,1,0:T(8,128)(2,1)S(1)}, bf16[4,72,512]{2,1,0:T(8,128)(2,1)S(1)}, u32[]{:S(2)}, u32[]{:S(2)}) collective-permute-start(bf16[4,72,512]{2,1,0:T(8,128)(2,1)S(1)} %pad_maximum_fusion), channel_id=1, source_target_pairs={{0,1},{1,2},{2,3},{4,5},{5,6},{6,7},{8,9},{9,10},{10,11},{12,13},{... | collective-permute-start | bytes 884744 | tf_op jit(solution)/shard_map/ppermute | solution.py:402
  15.6 19.9 %collective-permute-start.7 = (bf16[4,72,512]{2,1,0:T(8,128)(2,1)S(1)}, bf16[4,72,512]{2,1,0:T(8,128)(2,1)S(1)}, u32[]{:S(2)}, u32[]{:S(2)}) collective-permute-start(bf16[4,72,512]{2,1,0:T(8,128)(2,1)S(1)} %pad_maximum_fusion.1), channel_id=1, source_target_pairs={{1,0},{2,1},{3,2},{5,4},{6,5},{7,6},{9,8},{10,9},{11,10},{13,12},{... | collective-permute-start | bytes 884744 | tf_op jit(solution)/shard_map/ppermute | solution.py:403
  18.3 2.3 %copy-start.1 = (bf16[3,3,512,512]{3,2,1,0:T(8,128)(2,1)S(1)}, bf16[3,3,512,512]{3,2,1,0:T(8,128)(2,1)}, u32[]{:S(2)}) copy-start(bf16[3,3,512,512]{3,2,1,0:T(8,128)(2,1)} %refs_9_.1) | copy-start | bytes 14155780
  20.6 1.0 %copy-start.5 = (bf16[512,512]{1,0:T(8,128)(2,1)S(1)}, bf16[512,512]{1,0:T(8,128)(2,1)}, u32[]{:S(2)}) copy-start(bf16[512,512]{1,0:T(8,128)(2,1)} %refs_12_.3) | copy-start | bytes 1572868
  21.6 13.9 %copy-start.2 = (bf16[3,3,512,512]{3,2,1,0:T(8,128)(2,1)S(1)}, bf16[3,3,512,512]{3,2,1,0:T(8,128)(2,1)}, u32[]{:S(2)}) copy-start(bf16[3,3,512,512]{3,2,1,0:T(8,128)(2,1)} %refs_9_.1) | copy-start | bytes 14155780
  21.7 13.9 %copy-start.6 = (bf16[512,512]{1,0:T(8,128)(2,1)S(1)}, bf16[512,512]{1,0:T(8,128)(2,1)}, u32[]{:S(2)}) copy-start(bf16[512,512]{1,0:T(8,128)(2,1)} %refs_12_.3) | copy-start | bytes 1572868
  33.6 16.1 %collective-permute-start.11 = (bf16[2,4,16,512]{3,2,1,0:T(8,128)(2,1)S(1)}, bf16[2,4,16,512]{3,2,1,0:T(8,128)(2,1)S(1)}, u32[]{:S(2)}, u32[]{:S(2)}) collective-permute-start(bf16[2,4,16,512]{3,2,1,0:T(8,128)(2,1)S(1)} %get-tuple-element.34), channel_id=1, source_target_pairs={{0,4},{4,0},{8,12},{12,8},{1,5},{5,1},{9,13},{13,9},{2,6},{6,2},{1... | collective-permute-start | bytes 393224 | tf_op jit(solution)/shard_map/ppermute | solution.py:393
  33.8 15.9 %collective-permute-start.12 = (bf16[2,4,16,512]{3,2,1,0:T(8,128)(2,1)S(1)}, bf16[2,4,16,512]{3,2,1,0:T(8,128)(2,1)S(1)}, u32[]{:S(2)}, u32[]{:S(2)}) collective-permute-start(bf16[2,4,16,512]{3,2,1,0:T(8,128)(2,1)S(1)} %get-tuple-element.35), channel_id=1, source_target_pairs={{0,8},{4,12},{8,0},{12,4},{1,9},{5,13},{9,1},{13,5},{2,10},{6,14},... | collective-permute-start | bytes 393224 | tf_op jit(solution)/shard_map/ppermute | solution.py:393
  35.5 14.2 %collective-permute-start.13 = (bf16[2,4,16,512]{3,2,1,0:T(8,128)(2,1)S(1)}, bf16[2,4,16,512]{3,2,1,0:T(8,128)(2,1)S(1)}, u32[]{:S(2)}, u32[]{:S(2)}) collective-permute-start(bf16[2,4,16,512]{3,2,1,0:T(8,128)(2,1)S(1)} %get-tuple-element.36), channel_id=1, source_target_pairs={{0,12},{4,8},{8,4},{12,0},{1,13},{5,9},{9,5},{13,1},{2,14},{6,10},... | collective-permute-start | bytes 393224 | tf_op jit(solution)/shard_map/ppermute | solution.py:393
  47.5 2.2 %collective-permute-start.8 = (bf16[2,4,16,512]{3,2,1,0:T(8,128)(2,1)S(1)}, bf16[2,4,16,512]{3,2,1,0:T(8,128)(2,1)S(1)}, u32[]{:S(2)}, u32[]{:S(2)}) collective-permute-start(bf16[2,4,16,512]{3,2,1,0:T(8,128)(2,1)S(1)} %get-tuple-element.30), channel_id=1, source_target_pairs={{0,4},{4,0},{8,12},{12,8},{1,5},{5,1},{9,13},{13,9},{2,6},{6,2},{1... | collective-permute-start | bytes 393224 | tf_op jit(solution)/shard_map/ppermute | solution.py:393
  47.9 6.3 %collective-permute-start.9 = (bf16[2,4,16,512]{3,2,1,0:T(8,128)(2,1)S(1)}, bf16[2,4,16,512]{3,2,1,0:T(8,128)(2,1)S(1)}, u32[]{:S(2)}, u32[]{:S(2)}) collective-permute-start(bf16[2,4,16,512]{3,2,1,0:T(8,128)(2,1)S(1)} %get-tuple-element.31), channel_id=1, source_target_pairs={{0,8},{4,12},{8,0},{12,4},{1,9},{5,13},{9,1},{13,5},{2,10},{6,14},... | collective-permute-start | bytes 393224 | tf_op jit(solution)/shard_map/ppermute | solution.py:393
  49.7 5.8 %collective-permute-start.10 = (bf16[2,4,16,512]{3,2,1,0:T(8,128)(2,1)S(1)}, bf16[2,4,16,512]{3,2,1,0:T(8,128)(2,1)S(1)}, u32[]{:S(2)}, u32[]{:S(2)}) collective-permute-start(bf16[2,4,16,512]{3,2,1,0:T(8,128)(2,1)S(1)} %get-tuple-element.32), channel_id=1, source_target_pairs={{0,12},{4,8},{8,4},{12,0},{1,13},{5,9},{9,5},{13,1},{2,14},{6,10},... | collective-permute-start | bytes 393224 | tf_op jit(solution)/shard_map/ppermute | solution.py:393
